TPU v7x, 32 devices: a whole 2x2x4 slice. The times are simulated.
32 devices in a mesh: fsdp: 32 (over z, y, x, core).
Axes of the slice: x: 2, y: 2, z: 4, core: 2. Of those that a mesh axis runs over, the one named last changes fastest.
Arguments:
- tokens: bfloat16 [32768, 768], P('fsdp'), may hold values from -6 to 6
- cotangent: bfloat16 [32768, 128], P('fsdp'), may hold values from -6 to 6
- slot_row: int32 [32768], P('fsdp'), may hold values from 0 to 32767, as said below
- lengths: int32 [64], P('fsdp'), may hold values from 256 to 512, as said below
- w_qkv: bfloat16 [768, 2304], P('fsdp'), may hold values from -0.21875 to 0.21875
- b_qv: bfloat16 [1536], P('fsdp'), may hold values from -0.29882812 to 0.29882812
- w_out: bfloat16 [768, 768], P('fsdp'), may hold values from -4 to 4
- b_out: bfloat16 [768], P('fsdp'), may hold values from -1.796875 to 1.796875
- ln1_gain: bfloat16 [768], P('fsdp'), may hold values from 0.099609375 to 1.8984375
- ln1_bias: bfloat16 [768], P('fsdp'), may hold values from -1.796875 to 1.796875
- w_up: bfloat16 [768, 3072], P('fsdp'), may hold values from -0.21875 to 0.21875
- b_up: bfloat16 [3072], P('fsdp'), may hold values from -1.796875 to 1.796875
- w_down: bfloat16 [3072, 768], P('fsdp'), may hold values from -0.109375 to 0.109375
- b_down: bfloat16 [768], P('fsdp'), may hold values from -1.796875 to 1.796875
- ln2_gain: bfloat16 [768], P('fsdp'), may hold values from 0.099609375 to 1.8984375
- ln2_bias: bfloat16 [768], P('fsdp'), may hold values from -1.796875 to 1.796875
- w_proj: bfloat16 [768, 128], P('fsdp'), may hold values from -0.21875 to 0.21875
Outputs:
- embeddings: bfloat16 [32768, 128], P('fsdp')
- input_grad: bfloat16 [32768, 768], P('fsdp')
- grad_w_qkv: float32 [768, 2304], P('fsdp')
- grad_b_qv: float32 [1536], P('fsdp')
- grad_w_out: float32 [768, 768], P('fsdp')
- grad_b_out: float32 [768], P('fsdp')
- grad_ln1_gain: float32 [768], P('fsdp')
- grad_ln1_bias: float32 [768], P('fsdp')
- grad_w_up: float32 [768, 3072], P('fsdp')
- grad_b_up: float32 [3072], P('fsdp')
- grad_w_down: float32 [3072, 768], P('fsdp')
- grad_b_down: float32 [768], P('fsdp')
- grad_ln2_gain: float32 [768], P('fsdp')
- grad_ln2_bias: float32 [768], P('fsdp')
- grad_w_proj: float32 [768, 128], P('fsdp')
Inputs may be any that keep to these rules, and one draw needn't show every extreme that they name: slot_row is a permutation of the 32768 input rows. The 1024 slots of device k take exactly 32 rows from each device's shard of tokens, namely those whose position in that shard lies from k * 32 to (k + 1) * 32 - 1. Entries b * 2 to (b + 1) * 2 - 1 are the lengths of the passages laid one after another from the first slot of device b; the slots after them are padding. Some passage has exactly 512 tokens.
All inputs are finite; a program needn't handle non-finite values.
Results may differ from a plain program's by a relative error of at most 0.018.
Values may be sent and summed in bfloat16 or wider, within the bound.
A program may use at most 256 MiB of HBM per device.

v0:
```python
from functools import partial

import jax
import jax.numpy as jnp
from jax import lax
from jax.sharding import PartitionSpec as P

HEADS = 12
HEAD_DIM = 64


def passage_ids(length_block, row_count):
    position = jnp.arange(row_count, dtype=jnp.int32)
    bounds = jnp.cumsum(length_block)
    passage = jnp.sum((position[:, None] >= bounds[None, :]).astype(jnp.int32), axis=1)
    inside = passage < length_block.shape[0]
    passage = jnp.where(inside, passage, length_block.shape[0] + position)
    return (passage, inside)


def norm_parts(hidden):
    center = hidden - jnp.mean(hidden, axis=-1, keepdims=True)
    inverse = lax.rsqrt(jnp.mean(center * center, axis=-1, keepdims=True) + 1e-12)
    return (center * inverse, inverse)


def norm_back(grad_out, normed, inverse, gain):
    scaled = grad_out * gain
    centered = scaled - jnp.mean(scaled, axis=-1, keepdims=True)
    return inverse * (centered - normed * jnp.mean(scaled * normed, axis=-1, keepdims=True))


def head_view(matrix):
    return matrix.reshape(matrix.shape[0], HEADS, HEAD_DIM)


def masked_scores(query_block, keys_all, mask_block):
    scores = (
        jnp.einsum("qhd,khd->hqk", query_block, keys_all, preferred_element_type=jnp.float32)
        * 0.125
    )
    return jnp.where(mask_block[None], scores, -1e30)


def forward_pass(gathered, dealt, passage, inside):
    (
        w_qkv,
        b_qv,
        w_out,
        b_out,
        gain_one,
        bias_one,
        w_up,
        b_up,
        w_down,
        b_down,
        gain_two,
        bias_two,
        w_proj,
    ) = gathered
    row_count, model_width = dealt.shape
    key_zeros = jnp.zeros((model_width,), jnp.float32)
    bias_all = jnp.concatenate(
        [b_qv[:model_width].astype(jnp.float32), key_zeros, b_qv[model_width:].astype(jnp.float32)]
    )
    qkv_low = (jnp.dot(dealt, w_qkv, preferred_element_type=jnp.float32) + bias_all).astype(
        jnp.bfloat16
    )
    queries = head_view(qkv_low[:, :model_width])
    keys_all = head_view(qkv_low[:, model_width : 2 * model_width])
    values_all = head_view(qkv_low[:, 2 * model_width :])
    block_rows = min(512, row_count)

    def attend(block_index):
        first_row = block_index * block_rows
        query_block = lax.dynamic_slice_in_dim(queries, first_row, block_rows, 0)
        mask_block = (
            lax.dynamic_slice_in_dim(passage, first_row, block_rows, 0)[:, None] == passage[None, :]
        )
        scores = masked_scores(query_block, keys_all, mask_block)
        row_max = jnp.max(scores, axis=-1, keepdims=True)
        exponent = jnp.exp(scores - row_max)
        row_total = jnp.sum(exponent, axis=-1, keepdims=True)
        attn_low = (exponent / row_total).astype(jnp.bfloat16)
        context = jnp.einsum(
            "hqk,khd->qhd", attn_low, values_all, preferred_element_type=jnp.float32
        )
        return (context, (row_max + jnp.log(row_total))[..., 0])

    context, log_total = lax.map(attend, jnp.arange(row_count // block_rows))
    context_low = context.reshape(row_count, model_width).astype(jnp.bfloat16)
    hidden_one = (
        dealt.astype(jnp.float32)
        + jnp.dot(context_low, w_out, preferred_element_type=jnp.float32)
        + b_out.astype(jnp.float32)
    )
    normed_one, inverse_one = norm_parts(hidden_one)
    first_low = (normed_one * gain_one.astype(jnp.float32) + bias_one.astype(jnp.float32)).astype(
        jnp.bfloat16
    )
    up_input = jnp.dot(first_low, w_up, preferred_element_type=jnp.float32) + b_up.astype(
        jnp.float32
    )
    active_low = jax.nn.gelu(up_input, approximate=False).astype(jnp.bfloat16)
    hidden_two = (
        first_low.astype(jnp.float32)
        + jnp.dot(active_low, w_down, preferred_element_type=jnp.float32)
        + b_down.astype(jnp.float32)
    )
    normed_two, inverse_two = norm_parts(hidden_two)
    second_low = (normed_two * gain_two.astype(jnp.float32) + bias_two.astype(jnp.float32)).astype(
        jnp.bfloat16
    )
    project = jnp.dot(second_low, w_proj, preferred_element_type=jnp.float32)
    inv_norm = lax.rsqrt(jnp.sum(project * project, axis=-1, keepdims=True) + 1e-06)
    embedded = project * inv_norm * inside[:, None].astype(jnp.float32)
    kept = (
        queries,
        keys_all,
        values_all,
        log_total,
        context_low,
        normed_one,
        inverse_one,
        first_low,
        up_input,
        active_low,
        normed_two,
        inverse_two,
        second_low,
        project,
        inv_norm,
    )
    return (embedded, kept)


def upper_backward(gathered, dealt_cot, inside, kept):
    gain_one = gathered[4].astype(jnp.float32)
    w_up = gathered[6]
    w_down = gathered[8]
    gain_two = gathered[10].astype(jnp.float32)
    w_proj = gathered[12]
    normed_one, inverse_one, first_low, up_input, active_low = (
        kept[5],
        kept[6],
        kept[7],
        kept[8],
        kept[9],
    )
    normed_two, inverse_two, second_low, project, inv_norm = (
        kept[10],
        kept[11],
        kept[12],
        kept[13],
        kept[14],
    )
    grad_emb = dealt_cot.astype(jnp.float32) * inside[:, None].astype(jnp.float32)
    along = jnp.sum(project * grad_emb, axis=-1, keepdims=True)
    grad_project = (inv_norm * grad_emb - inv_norm * inv_norm * inv_norm * along * project).astype(
        jnp.bfloat16
    )
    grad_w_proj = jnp.einsum(
        "sd,se->de", second_low, grad_project, preferred_element_type=jnp.float32
    )
    grad_second = jnp.einsum("se,de->sd", grad_project, w_proj, preferred_element_type=jnp.float32)
    grad_gain_two = jnp.sum(grad_second * normed_two, axis=0)
    grad_bias_two = jnp.sum(grad_second, axis=0)
    grad_hidden_two = norm_back(grad_second, normed_two, inverse_two, gain_two)
    grad_b_down = jnp.sum(grad_hidden_two, axis=0)
    down_low = grad_hidden_two.astype(jnp.bfloat16)
    grad_w_down = jnp.einsum("sf,sd->fd", active_low, down_low, preferred_element_type=jnp.float32)
    grad_active = jnp.einsum("sd,fd->sf", down_low, w_down, preferred_element_type=jnp.float32)
    gelu_value, gelu_back = jax.vjp(partial(jax.nn.gelu, approximate=False), up_input)
    grad_up = gelu_back(grad_active)[0]
    grad_b_up = jnp.sum(grad_up, axis=0)
    up_low = grad_up.astype(jnp.bfloat16)
    grad_w_up = jnp.einsum("sd,sf->df", first_low, up_low, preferred_element_type=jnp.float32)
    grad_first = grad_hidden_two + jnp.einsum(
        "sf,df->sd", up_low, w_up, preferred_element_type=jnp.float32
    )
    grad_gain_one = jnp.sum(grad_first * normed_one, axis=0)
    grad_bias_one = jnp.sum(grad_first, axis=0)
    grad_hidden_one = norm_back(grad_first, normed_one, inverse_one, gain_one)
    upper_grads = (
        grad_gain_one,
        grad_bias_one,
        grad_w_up,
        grad_b_up,
        grad_w_down,
        grad_b_down,
        grad_gain_two,
        grad_bias_two,
        grad_w_proj,
    )
    return (upper_grads, grad_hidden_one)


def lower_backward(gathered, dealt, passage, kept, grad_hidden_one):
    w_qkv = gathered[0]
    w_out = gathered[2]
    queries, keys_all, values_all, log_total, context_low = (
        kept[0],
        kept[1],
        kept[2],
        kept[3],
        kept[4],
    )
    row_count, model_width = dealt.shape
    grad_b_out = jnp.sum(grad_hidden_one, axis=0)
    out_low = grad_hidden_one.astype(jnp.bfloat16)
    grad_w_out = jnp.einsum("sd,se->de", context_low, out_low, preferred_element_type=jnp.float32)
    grad_context = head_view(
        jnp.einsum("se,de->sd", out_low, w_out, preferred_element_type=jnp.float32).astype(
            jnp.bfloat16
        )
    )
    block_rows = min(512, row_count)

    def attend_back(carry, block_index):
        grad_keys, grad_values = carry
        first_row = block_index * block_rows
        query_block = lax.dynamic_slice_in_dim(queries, first_row, block_rows, 0)
        grad_block = lax.dynamic_slice_in_dim(grad_context, first_row, block_rows, 0)
        mask_block = (
            lax.dynamic_slice_in_dim(passage, first_row, block_rows, 0)[:, None] == passage[None, :]
        )
        scores = masked_scores(query_block, keys_all, mask_block)
        attn_probs = jnp.exp(scores - log_total[block_index][..., None])
        attn_low = attn_probs.astype(jnp.bfloat16)
        grad_values = grad_values + jnp.einsum(
            "hqk,qhd->khd", attn_low, grad_block, preferred_element_type=jnp.float32
        )
        grad_probs = jnp.einsum(
            "qhd,khd->hqk", grad_block, values_all, preferred_element_type=jnp.float32
        )
        grad_scores = (
            attn_probs * (grad_probs - jnp.sum(attn_probs * grad_probs, axis=-1, keepdims=True))
        ).astype(jnp.bfloat16)
        grad_query = (
            jnp.einsum("hqk,khd->qhd", grad_scores, keys_all, preferred_element_type=jnp.float32)
            * 0.125
        )
        grad_keys = (
            grad_keys
            + jnp.einsum(
                "hqk,qhd->khd", grad_scores, query_block, preferred_element_type=jnp.float32
            )
            * 0.125
        )
        return ((grad_keys, grad_values), grad_query)

    zero_heads = jnp.zeros(keys_all.shape, jnp.float32)
    (grad_keys, grad_values), grad_queries = lax.scan(
        attend_back, (zero_heads, zero_heads), jnp.arange(row_count // block_rows)
    )
    grad_queries = grad_queries.reshape(row_count, model_width)
    grad_values = grad_values.reshape(row_count, model_width)
    grad_qkv = jnp.concatenate(
        [grad_queries, grad_keys.reshape(row_count, model_width), grad_values], axis=1
    )
    grad_b_qv = jnp.concatenate([jnp.sum(grad_queries, axis=0), jnp.sum(grad_values, axis=0)])
    qkv_low_grad = grad_qkv.astype(jnp.bfloat16)
    grad_w_qkv = jnp.einsum("sd,sc->dc", dealt, qkv_low_grad, preferred_element_type=jnp.float32)
    grad_dealt = (
        jnp.einsum("sc,dc->sd", qkv_low_grad, w_qkv, preferred_element_type=jnp.float32)
        + grad_hidden_one
    )
    return ((grad_w_qkv, grad_b_qv, grad_w_out, grad_b_out), grad_dealt)


def local(
    tokens,
    cotangent,
    slot_row,
    lengths,
    w_qkv,
    b_qv,
    w_out,
    b_out,
    ln1_gain,
    ln1_bias,
    w_up,
    b_up,
    w_down,
    b_down,
    ln2_gain,
    ln2_bias,
    w_proj,
):
    devices = lax.axis_size("fsdp")
    row_count = tokens.shape[0]
    peer_rows = row_count // devices
    arrived, arrived_cot = (
        lax.all_to_all(tokens, "fsdp", split_axis=0, concat_axis=0, tiled=True),
        lax.all_to_all(cotangent, "fsdp", split_axis=0, concat_axis=0, tiled=True),
    )
    local_row = slot_row // row_count * peer_rows + slot_row % peer_rows
    dealt = arrived[local_row]
    dealt_cot = arrived_cot[local_row]
    passage, inside = passage_ids(lengths, row_count)
    gathered = (
        lax.all_gather(w_qkv, "fsdp", axis=0, tiled=True),
        lax.all_gather(b_qv, "fsdp", axis=0, tiled=True),
        lax.all_gather(w_out, "fsdp", axis=0, tiled=True),
        lax.all_gather(b_out, "fsdp", axis=0, tiled=True),
        lax.all_gather(ln1_gain, "fsdp", axis=0, tiled=True),
        lax.all_gather(ln1_bias, "fsdp", axis=0, tiled=True),
        lax.all_gather(w_up, "fsdp", axis=0, tiled=True),
        lax.all_gather(b_up, "fsdp", axis=0, tiled=True),
        lax.all_gather(w_down, "fsdp", axis=0, tiled=True),
        lax.all_gather(b_down, "fsdp", axis=0, tiled=True),
        lax.all_gather(ln2_gain, "fsdp", axis=0, tiled=True),
        lax.all_gather(ln2_bias, "fsdp", axis=0, tiled=True),
        lax.all_gather(w_proj, "fsdp", axis=0, tiled=True),
    )
    embedded, kept = forward_pass(gathered, dealt, passage, inside)
    gathered = (
        lax.all_gather(w_qkv, "fsdp", axis=0, tiled=True),
        lax.all_gather(b_qv, "fsdp", axis=0, tiled=True),
        lax.all_gather(w_out, "fsdp", axis=0, tiled=True),
        lax.all_gather(b_out, "fsdp", axis=0, tiled=True),
        lax.all_gather(ln1_gain, "fsdp", axis=0, tiled=True),
        lax.all_gather(ln1_bias, "fsdp", axis=0, tiled=True),
        lax.all_gather(w_up, "fsdp", axis=0, tiled=True),
        lax.all_gather(b_up, "fsdp", axis=0, tiled=True),
        lax.all_gather(w_down, "fsdp", axis=0, tiled=True),
        lax.all_gather(b_down, "fsdp", axis=0, tiled=True),
        lax.all_gather(ln2_gain, "fsdp", axis=0, tiled=True),
        lax.all_gather(ln2_bias, "fsdp", axis=0, tiled=True),
        lax.all_gather(w_proj, "fsdp", axis=0, tiled=True),
    )
    embedded_again, kept = forward_pass(gathered, dealt, passage, inside)
    upper_grads, grad_hidden_one = upper_backward(gathered, dealt_cot, inside, kept)
    (
        grad_gain_one,
        grad_bias_one,
        grad_w_up,
        grad_b_up,
        grad_w_down,
        grad_b_down,
        grad_gain_two,
        grad_bias_two,
        grad_w_proj,
    ) = upper_grads
    lower_grads, grad_dealt = lower_backward(gathered, dealt, passage, kept, grad_hidden_one)
    grad_w_qkv, grad_b_qv, grad_w_out, grad_b_out = lower_grads
    all_shards = (
        lax.psum_scatter(grad_w_qkv, "fsdp", scatter_dimension=0, tiled=True),
        lax.psum_scatter(grad_b_qv, "fsdp", scatter_dimension=0, tiled=True),
        lax.psum_scatter(grad_w_out, "fsdp", scatter_dimension=0, tiled=True),
        lax.psum_scatter(grad_b_out, "fsdp", scatter_dimension=0, tiled=True),
        lax.psum_scatter(grad_gain_one, "fsdp", scatter_dimension=0, tiled=True),
        lax.psum_scatter(grad_bias_one, "fsdp", scatter_dimension=0, tiled=True),
        lax.psum_scatter(grad_w_up, "fsdp", scatter_dimension=0, tiled=True),
        lax.psum_scatter(grad_b_up, "fsdp", scatter_dimension=0, tiled=True),
        lax.psum_scatter(grad_w_down, "fsdp", scatter_dimension=0, tiled=True),
        lax.psum_scatter(grad_b_down, "fsdp", scatter_dimension=0, tiled=True),
        lax.psum_scatter(grad_gain_two, "fsdp", scatter_dimension=0, tiled=True),
        lax.psum_scatter(grad_bias_two, "fsdp", scatter_dimension=0, tiled=True),
        lax.psum_scatter(grad_w_proj, "fsdp", scatter_dimension=0, tiled=True),
    )
    lower_shards = all_shards[:4]
    upper_shards = all_shards[4:]
    inverse_row = (
        jnp.zeros((row_count,), jnp.int32).at[local_row].set(jnp.arange(row_count, dtype=jnp.int32))
    )
    emb_low = embedded.astype(jnp.bfloat16)[inverse_row]
    dealt_grad_low = grad_dealt.astype(jnp.bfloat16)[inverse_row]
    returned_emb, returned_grad = (
        lax.all_to_all(emb_low, "fsdp", split_axis=0, concat_axis=0, tiled=True),
        lax.all_to_all(dealt_grad_low, "fsdp", split_axis=0, concat_axis=0, tiled=True),
    )
    return (
        returned_emb,
        returned_grad,
        lower_shards[0],
        lower_shards[1],
        lower_shards[2],
        lower_shards[3],
        upper_shards[0],
        upper_shards[1],
        upper_shards[2],
        upper_shards[3],
        upper_shards[4],
        upper_shards[5],
        upper_shards[6],
        upper_shards[7],
        upper_shards[8],
    )


def solution(mesh):
    in_specs = (
        P("fsdp", None),
        P("fsdp", None),
        P("fsdp"),
        P("fsdp"),
        P("fsdp", None),
        P("fsdp"),
        P("fsdp", None),
        P("fsdp"),
        P("fsdp"),
        P("fsdp"),
        P("fsdp", None),
        P("fsdp"),
        P("fsdp", None),
        P("fsdp"),
        P("fsdp"),
        P("fsdp"),
        P("fsdp", None),
    )
    out_specs = (
        P("fsdp", None),
        P("fsdp", None),
        P("fsdp", None),
        P("fsdp"),
        P("fsdp", None),
        P("fsdp"),
        P("fsdp"),
        P("fsdp"),
        P("fsdp", None),
        P("fsdp"),
        P("fsdp", None),
        P("fsdp"),
        P("fsdp"),
        P("fsdp"),
        P("fsdp", None),
    )
    return jax.shard_map(local, mesh=mesh, in_specs=in_specs, out_specs=out_specs, check_vma=False)
```

profile of v0, /device:TPU:18, one launch (start us, length us, event | category | flops | bytes accessed | tf_op | source)
XLA Modules:
  0.0 1155.1 jit_solution(333526717605930837)
XLA Ops:
  9.4 13.7 %all_to_all.48 = bf16[32,32,128]{2,1,0:T(8,128)(2,1)S(1)} all-to-all(bf16[32,32,128]{2,1,0:T(8,128)(2,1)} %bitcast.177), channel_id=1, replica_groups=mesh['fsdp'=32] {'fsdp'}, dimensions={0} | all-to-all | bytes 524288 | tf_op jit(solution)/shard_map/all_to_all | solution.py:295
  34.1 65.8 %all-reduce.18 = (bf16[1536]{0:T(1024)(128)(2,1)S(1)}, bf16[768]{0:T(1024)(128)(2,1)S(1)}, bf16[768]{0:T(1024)(128)(2,1)S(1)}, bf16[768]{0:T(1024)(128)(2,1)S(1)...) all-reduce(bf16[1536]{0:T(1024)(128)(2,1)S(1)} %dynamic-update-slic, ...), channel_id=1, replica_groups=mesh['fsdp'=32] {'fsdp'}, use_global_device_ids=true, to_apply=%add | all-reduce | flops 9216 | bytes 36864
  104.1 32.8 %all_gather.64 = bf16[768,128]{1,0:T(8,128)(2,1)} all-gather(bf16[24,128]{1,0:T(8,128)(2,1)S(1)} %copy-done.48), channel_id=1, replica_groups=mesh['fsdp'=32] {'fsdp'}, dimensions={0}, use_global_device_ids=true | all-gather | bytes 202752 | tf_op jit(solution)/shard_map/all_gather | solution.py:314
  161.3 117.2 %while.40 = (s32[]{:T(128)}, bf16[2,512,12,64]{1,3,2,0:T(8,128)(2,1)}, s32[2]{0:T(128)S(1)}, s32[1024]{0:T(1024)S(1)}, bf16[1024,12,64]{0,2,1:T(8,128)(2,1)S(1)}...) while((s32[]{:T(128)}, ...), condition=%wide.region_5.6_spmd.clone, body=%wide.region_2.5_spmd.sunk.clone | while | flops 1661469696 | bytes 107276952 | solution.py:90
  174.0 34.0 %fusion.220 = (f32[12,512]{1,0:T(8,128)S(1)}, f32[12,512,1024]{2,1,0:T(8,128)}) fusion(f32[12,512,1024]{2,1,0:T(8,128)} %fusion.219, pred[512,1024]{1,0:T(8,128)(4,1)} %broadcast_compare_fusion.9), kind=kOutput, calls=%fused_computation.220.clone.1.clone | output fusion | flops 37749760 | bytes 50880512 | tf_op jit(solution)/shard_map/while/body/eval_jaxpr/sub | solution.py:82
  208.0 11.8 %bitcast_dynamic-update-slice_fusion.12 = bf16[2,512,12,64]{1,3,2,0:T(8,128)(2,1)} fusion(bf16[2,512,12,64]{1,3,2,0:T(8,128)(2,1)} %get-tuple-element.633, s32[]{:T(128)} %get-tuple-element.632, bf16[1024,12,64]{0,2,1:T(8,128)(2,1)} %get-tuple-element.646, f32[12,512,1024]{2,1,0:T(8,128)} %get-tuple-element.528, ...), kind=kOutput, calls=%fused_computation.14.clone.1.clone | convolution fusion | flops 817889280 | bytes 28336640 | tf_op jit(solution)/shard_map/while/body/eval_jaxpr/hqk,khd->qhd/dot_general | solution.py:85
  232.6 33.9 %fusion.220 = (f32[12,512]{1,0:T(8,128)S(1)}, f32[12,512,1024]{2,1,0:T(8,128)}) fusion(f32[12,512,1024]{2,1,0:T(8,128)} %fusion.219, pred[512,1024]{1,0:T(8,128)(4,1)} %broadcast_compare_fusion.9), kind=kOutput, calls=%fused_computation.220.clone.1.clone | output fusion | flops 37749760 | bytes 50880512 | tf_op jit(solution)/shard_map/while/body/eval_jaxpr/sub | solution.py:82
  289.7 72.5 %while.41 = (s32[]{:T(128)}, bf16[2,512,12,64]{1,3,2,0:T(8,128)(2,1)}, f32[2,12,512]{2,1,0:T(8,128)}, s32[2]{0:T(128)S(1)}, s32[1024]{0:T(1024)S(1)}, /*index=5*...) while((s32[]{:T(128)}, ...), condition=%wide.region_15.16_spmd.clone, body=%wide.region_12.15_spmd.sunk.clone | while | flops 1686628352 | bytes 190270672 | solution.py:90
  302.1 12.3 %fusion.224 = f32[12,512]{1,0:T(8,128)S(1)} fusion(f32[12,512,1024]{2,1,0:T(8,128)} %get-tuple-element.552, f32[12,512]{1,0:T(8,128)S(1)} %get-tuple-element.553, pred[512,1024]{1,0:T(8,128)(4,1)S(1)} %broadcast_compare_fusion.10), kind=kLoop, calls=%fused_computation.25.clone.1.clone | loop fusion | flops 25159680 | bytes 25739264 | tf_op jit(solution)/shard_map/while/body/eval_jaxpr/reduce_sum | solution.py:83
  338.4 12.3 %fusion.224 = f32[12,512]{1,0:T(8,128)S(1)} fusion(f32[12,512,1024]{2,1,0:T(8,128)} %get-tuple-element.552, f32[12,512]{1,0:T(8,128)S(1)} %get-tuple-element.553, pred[512,1024]{1,0:T(8,128)(4,1)S(1)} %broadcast_compare_fusion.10), kind=kLoop, calls=%fused_computation.25.clone.1.clone | loop fusion | flops 25159680 | bytes 25739264 | tf_op jit(solution)/shard_map/while/body/eval_jaxpr/reduce_sum | solution.py:83
  370.9 37.2 %fusion.64.clone.4 = bf16[1024,3072]{1,0:T(8,128)(2,1)} fusion(f32[3072]{0:T(1024)S(1)} %copy-done.46, bf16[768,3072]{1,0:T(8,128)(2,1)} %all-gather.9.cloned.1.call-done, f32[1024,768]{0,1:T(8,128)} %copy-done.16, f32[768]{0:T(1024)S(1)} %copy-done.50, f32[768]{0:T(1024)S(1)} %copy-done.34, f32[1024]{0:T(1024)S(1)} %copy-done.55, ...), kind=kOutput, calls=%fused_computation.62.clone.clone.clone.clone.clone.clone.1 | convolution fusion | flops 5043388416 | bytes 14182400 | tf_op jit(solution)/shard_map/dot_general | solution.py:101
  418.2 35.9 %multiply_convert_fusion.1 = (bf16[1024,3072]{1,0:T(8,128)(2,1)}, f32[1024,3072]{1,0:T(8,128)}, f32[1024,3072]{1,0:T(8,128)}) fusion(f32[3072]{0:T(1024)S(1)} %copy-done.46, bf16[768,3072]{1,0:T(8,128)(2,1)S(1)} %copy-done.58, f32[1024,768]{0,1:T(8,128)S(1)} %copy-done.9, f32[1024]{0:T(1024)S(1)} %add_rsqrt_fusion.2, ...), kind=kOutput, calls=%fused_computation.65 | convolution fusion | flops 5043388416 | bytes 39348224 | tf_op jit(solution)/shard_map/dot_general | solution.py:101
  481.7 19.8 %fusion.130 = (f32[3072]{0:T(1024)}, bf16[1024,3072]{1,0:T(8,128)(2,1)}) fusion(f32[1024,3072]{1,0:T(8,128)} %get-tuple-element.304, bf16[3072,768]{1,0:T(8,128)(2,1)} %all-gather.11.cloned.1.call-done, f32[1024,768]{0,1:T(8,128)} %get-tuple-element.300, f32[1024,3072]{1,0:T(8,128)} %get-tuple-element.330, f32[3072]{0:T(1024)S(1)} %copy-done.46), kind=kOutput, calls=%fused_computation.229 | convolution fusion | flops 4882953216 | bytes 39346176 | tf_op jit(solution)/shard_map/sd,fd->sf/dot_general | solution.py:172
  523.5 177.7 %while.42 = (s32[]{:T(128)}, f32[1024,12,64]{0,2,1:T(8,128)}, f32[1024,12,64]{0,2,1:T(8,128)}, f32[2,512,12,64]{1,3,2,0:T(8,128)}, s32[2]{0:T(128)S(1)}, /*index...) while((s32[]{:T(128)}, f32[1024,12,64]{0,2,1:T(8,128)}, ...), condition=%wide.region_28.29_spmd.clone.clone, body=%wide.region_26.28_spmd.clone.sunk.clone | while | flops 4125747200 | bytes 213043952 | solution.py:253
  538.6 18.3 %multiply_reduce_fusion.16 = (f32[12,512]{1,0:T(8,128)S(1)}, f32[12,512,1024]{2,1,0:T(8,128)}) fusion(f32[12,512,1024]{2,1,0:T(8,128)} %fusion.234, f32[12,512]{1,0:T(8,128)S(1)} %dynamic-slice_bitcast_fusion.3, pred[512,1024]{1,0:T(8,128)(4,1)} %broadcast_compare_fusion.11, bf16[1024,12,64]{0,2,1:T(8,128)(2,1)} %get-tuple-element.680, ...), kind=kOutput, calls=%fused_computation.36.clone.1.clone | convolution fusion | flops 836757504 | bytes 53264388 | tf_op jit(solution)/shard_map/while/body/eval_jaxpr/qhd,khd->hqk/dot_general | solution.py:233
  557.0 22.3 %multiply_convert_fusion.5 = bf16[12,512,1024]{2,1,0:T(8,128)(2,1)} fusion(f32[12,512,1024]{2,1,0:T(8,128)} %get-tuple-element.579, f32[12,512,1024]{2,1,0:T(8,128)} %fusion.234, f32[12,512]{1,0:T(8,128)S(1)} %get-tuple-element.580, f32[12,512]{1,0:T(8,128)S(1)} %dynamic-slice_bitcast_fusion.3, pred[512,1024]{1,0:T(8,128)(4,1)} %broadcast_compare_fusion.11), kind=kLoop, calls=%fused_computation.35.clone.1.clone | loop fusion | flops 37748736 | bytes 63488000 | tf_op jit(solution)/shard_map/while/body/eval_jaxpr/convert_element_type | solution.py:238
  597.7 14.1 %bitcast_add_fusion.7 = f32[1024,12,64]{0,2,1:T(8,128)} fusion(f32[1024,12,64]{0,2,1:T(8,128)} %get-tuple-element.661, f32[12,512,1024]{2,1,0:T(8,128)} %fusion.234, f32[12,512]{1,0:T(8,128)S(1)} %dynamic-slice_bitcast_fusion.3, pred[512,1024]{1,0:T(8,128)(4,1)} %broadcast_compare_fusion.11, pred[]{:T(512)S(6)} %compare.7, ...), kind=kOutput, calls=%fused_computation.41.clone.1.clone | convolution fusion | flops 832045056 | bytes 32792580 | tf_op jit(solution)/shard_map/while/body/eval_jaxpr/hqk,qhd->khd/dot_general | solution.py:230
  626.5 18.2 %multiply_reduce_fusion.16 = (f32[12,512]{1,0:T(8,128)S(1)}, f32[12,512,1024]{2,1,0:T(8,128)}) fusion(f32[12,512,1024]{2,1,0:T(8,128)} %fusion.234, f32[12,512]{1,0:T(8,128)S(1)} %dynamic-slice_bitcast_fusion.3, pred[512,1024]{1,0:T(8,128)(4,1)} %broadcast_compare_fusion.11, bf16[1024,12,64]{0,2,1:T(8,128)(2,1)} %get-tuple-element.680, ...), kind=kOutput, calls=%fused_computation.36.clone.1.clone | convolution fusion | flops 836757504 | bytes 53264388 | tf_op jit(solution)/shard_map/while/body/eval_jaxpr/qhd,khd->hqk/dot_general | solution.py:233
  644.8 22.4 %multiply_convert_fusion.5 = bf16[12,512,1024]{2,1,0:T(8,128)(2,1)} fusion(f32[12,512,1024]{2,1,0:T(8,128)} %get-tuple-element.579, f32[12,512,1024]{2,1,0:T(8,128)} %fusion.234, f32[12,512]{1,0:T(8,128)S(1)} %get-tuple-element.580, f32[12,512]{1,0:T(8,128)S(1)} %dynamic-slice_bitcast_fusion.3, pred[512,1024]{1,0:T(8,128)(4,1)} %broadcast_compare_fusion.11), kind=kLoop, calls=%fused_computation.35.clone.1.clone | loop fusion | flops 37748736 | bytes 63488000 | tf_op jit(solution)/shard_map/while/body/eval_jaxpr/convert_element_type | solution.py:238
  686.5 14.6 %bitcast_add_fusion.7 = f32[1024,12,64]{0,2,1:T(8,128)} fusion(f32[1024,12,64]{0,2,1:T(8,128)} %get-tuple-element.661, f32[12,512,1024]{2,1,0:T(8,128)} %fusion.234, f32[12,512]{1,0:T(8,128)S(1)} %dynamic-slice_bitcast_fusion.3, pred[512,1024]{1,0:T(8,128)(4,1)} %broadcast_compare_fusion.11, pred[]{:T(512)S(6)} %compare.7, ...), kind=kOutput, calls=%fused_computation.41.clone.1.clone | convolution fusion | flops 832045056 | bytes 32792580 | tf_op jit(solution)/shard_map/while/body/eval_jaxpr/hqk,qhd->khd/dot_general | solution.py:230
  755.0 16.2 %all-to-all-start.1 = ((bf16[32,32,128]{2,1,0:T(8,128)(2,1)}), bf16[32,32,128]{2,1,0:T(8,128)(2,1)}, u32[]{:S(2)}, u32[]{:S(2)}) async-start(bf16[32,32,128]{2,1,0:T(8,128)(2,1)} %bitcast.176), calls=%async_computation.1 | async-start | bytes 524288 | tf_op jit(solution)/shard_map/all_to_all | solution.py:370
  793.0 74.6 %all-reduce.17 = (f32[1536]{0:T(1024)S(1)}, f32[768]{0:T(1024)S(1)}, f32[768]{0:T(1024)S(1)}, f32[768]{0:T(1024)S(1)}, f32[3072]{0:T(1024)S(1)}, /*index=5*/f32[...) all-reduce(f32[1536]{0:T(1024)S(1)} %pad_maximum_fusion.6, ...), channel_id=3, replica_groups=mesh['fsdp'=32] {'fsdp'}, use_global_device_ids=true, to_apply=%region_32.33.clone | all-reduce | flops 9216 | bytes 73728
  872.4 131.5 %reduce-scatter.14.cloned.1.call-done = f32[96,768]{1,0:T(8,128)} async-done(((f32[3072,768]{1,0:T(8,128)}), f32[96,768]{1,0:T(8,128)}) %reduce-scatter.14.cloned.1.call-update) | async-done | bytes 294928 | tf_op jit(solution)/shard_map/reduce_scatter | solution.py:356
  1003.9 141.6 %reduce-scatter.12.cloned.1.call-done = f32[24,3072]{1,0:T(8,128)} async-done(((f32[768,3072]{1,0:T(8,128)}), f32[24,3072]{1,0:T(8,128)}) %reduce-scatter.12.cloned.1.call-update) | async-done | bytes 294928 | tf_op jit(solution)/shard_map/reduce_scatter | solution.py:354
  (328 shorter events, 347.5 us)
Async XLA Ops:
  7.2 141.0 %all-gather.5.cloned.1.call-start = ((), (), s32[]{:S(2)}) async-start(), calls=%async_computation.9 | async-start | bytes 3649536 | tf_op jit(solution)/shard_map/all_gather | solution.py:302
  7.9 275.3 %all-gather.7.cloned.1.call-start = ((), (), s32[]{:S(2)}) async-start(), calls=%async_computation.10 | async-start | bytes 1216512 | tf_op jit(solution)/shard_map/all_gather | solution.py:304
  8.7 362.1 %all-gather.9.cloned.1.call-start = ((), (), s32[]{:S(2)}) async-start(), calls=%async_computation.11 | async-start | bytes 4866048 | tf_op jit(solution)/shard_map/all_gather | solution.py:308
  23.2 80.9 %copy-start.48 = (bf16[24,128]{1,0:T(8,128)(2,1)S(1)}, bf16[24,128]{1,0:T(8,128)(2,1)}, u32[]{:S(2)}) copy-start(bf16[24,128]{1,0:T(8,128)(2,1)} %param.39) | copy-start | bytes 18436
  23.2 114.4 %copy-start.49 = (s32[1024]{0:T(1024)S(1)}, s32[1024]{0:T(1024)}, u32[]{:S(2)}) copy-start(s32[1024]{0:T(1024)} %param.25) | copy-start | bytes 12292
  23.2 119.2 %all-to-all-start = ((bf16[32,32,768]{2,1,0:T(8,128)(2,1)}), bf16[32,32,768]{2,1,0:T(8,128)(2,1)S(1)}, u32[]{:S(2)}, u32[]{:S(2)}) async-start(bf16[32,32,768]{2,1,0:T(8,128)(2,1)} %bitcast.166), calls=%async_computation | async-start | bytes 3145728 | tf_op jit(solution)/shard_map/all_to_all | solution.py:294
  28.9 379.2 %all-gather.11.cloned.1.call-start = ((), (), s32[]{:S(2)}) async-start(), calls=%async_computation.12 | async-start | bytes 4866048 | tf_op jit(solution)/shard_map/all_gather | solution.py:310
  29.5 842.9 %reduce-scatter.16.cloned.1.call-start = ((), (), s32[]{:S(2)}) async-start(), calls=%async_computation.17 | async-start | bytes 405504
  291.4 23.6 %copy-start.6 = (bf16[1024,12,64]{0,2,1:T(8,128)(2,1)S(1)}, bf16[1024,12,64]{0,2,1:T(8,128)(2,1)}, u32[]{:S(2)}) copy-start(bf16[1024,12,64]{0,2,1:T(8,128)(2,1)} %get-tuple-element.622) | copy-start | bytes 4718596 | tf_op jit(solution)/shard_map/while
  327.7 23.6 %copy-start.6 = (bf16[1024,12,64]{0,2,1:T(8,128)(2,1)S(1)}, bf16[1024,12,64]{0,2,1:T(8,128)(2,1)}, u32[]{:S(2)}) copy-start(bf16[1024,12,64]{0,2,1:T(8,128)(2,1)} %get-tuple-element.622) | copy-start | bytes 4718596 | tf_op jit(solution)/shard_map/while
  368.7 143.5 %copy-start.32 = (f32[1024]{0:T(1024)}, f32[1024]{0:T(1024)S(1)}, u32[]{:S(2)}) copy-start(f32[1024]{0:T(1024)S(1)} %broadcast_multiply_fusion.5) | copy-start | bytes 12292
  370.8 141.4 %copy-start.36 = (f32[1024]{0:T(1024)}, f32[1024]{0:T(1024)S(1)}, u32[]{:S(2)}) copy-start(f32[1024]{0:T(1024)S(1)} %add_rsqrt_fusion.2) | copy-start | bytes 12292
  370.8 37.3 %copy-start.52 = (f32[768]{0:T(1024)S(1)}, f32[768]{0:T(1024)}, u32[]{:S(2)}) copy-start(f32[768]{0:T(1024)} %convert_element_type.145) | copy-start | bytes 9220
  408.1 45.9 %slice-start = ((s8[4718592]{0:T(1024)(128)(4,1)}), s8[4194304]{0:T(1024)(128)(4,1)S(1)}, s32[]{:S(2)}) async-start(s8[4718592]{0:T(1024)(128)(4,1)} %bitcast.179), calls=%async_computation.18 | async-start | bytes 8388608
  418.1 35.9 %copy-start.10 = (f32[1024,768]{0,1:T(8,128)S(1)}, f32[1024,768]{0,1:T(8,128)}, u32[]{:S(2)}) copy-start(f32[1024,768]{0,1:T(8,128)} %copy-done.8) | copy-start | bytes 9437188
  418.2 35.9 %slice-start.1 = ((s8[4718592]{0:T(1024)(128)(4,1)}), s8[524288]{0:T(1024)(128)(4,1)S(1)}, s32[]{:S(2)}) async-start(s8[4718592]{0:T(1024)(128)(4,1)} %bitcast.179), calls=%async_computation.19 | async-start | bytes 1048576
  476.3 396.0 %reduce-scatter.10.cloned.1.call-start = ((), (), s32[]{:S(2)}) async-start(), calls=%async_computation.14 | async-start | bytes 2433024 | tf_op jit(solution)/shard_map/reduce_scatter | solution.py:350
  481.7 19.8 %copy-start.11 = (f32[1024,768]{0,1:T(8,128)S(1)}, f32[1024,768]{0,1:T(8,128)}, u32[]{:S(2)}) copy-start(f32[1024,768]{0,1:T(8,128)} %copy-done.8) | copy-start | bytes 9437188
  518.5 353.9 %reduce-scatter.8.cloned.1.call-start = ((), (), s32[]{:S(2)}) async-start(), calls=%async_computation.13 | async-start | bytes 7299072 | tf_op jit(solution)/shard_map/reduce_scatter | solution.py:348
  720.2 283.7 %reduce-scatter.14.cloned.1.call-start = ((), (), s32[]{:S(2)}) async-start(), calls=%async_computation.16 | async-start | bytes 9732096 | tf_op jit(solution)/shard_map/reduce_scatter | solution.py:356
  732.4 413.1 %reduce-scatter.12.cloned.1.call-start = ((), (), s32[]{:S(2)}) async-start(), calls=%async_computation.15 | async-start | bytes 9732096 | tf_op jit(solution)/shard_map/reduce_scatter | solution.py:354
  745.0 26.3 %copy-start.18 = (f32[1024,768]{0,1:T(8,128)S(1)}, f32[1024,768]{0,1:T(8,128)}, u32[]{:S(2)}) copy-start(f32[1024,768]{0,1:T(8,128)} %copy-done.17) | copy-start | bytes 9437188
  755.0 32.0 %all-to-all-start.1 = ((bf16[32,32,128]{2,1,0:T(8,128)(2,1)}), bf16[32,32,128]{2,1,0:T(8,128)(2,1)}, u32[]{:S(2)}, u32[]{:S(2)}) async-start(bf16[32,32,128]{2,1,0:T(8,128)(2,1)} %bitcast.176), calls=%async_computation.1 | async-start | bytes 524288 | tf_op jit(solution)/shard_map/all_to_all | solution.py:370
  787.0 85.3 %all-to-all-start.3 = ((bf16[32,32,768]{2,1,0:T(8,128)(2,1)}), bf16[32,32,768]{2,1,0:T(8,128)(2,1)S(1)}, u32[]{:S(2)}, u32[]{:S(2)}) async-start(bf16[32,32,768]{2,1,0:T(8,128)(2,1)} %bitcast.21), calls=%async_computation.3 | async-start | bytes 3145728 | tf_op jit(solution)/shard_map/all_to_all | solution.py:371
  (61 other events, 363.9 us)
Sparse Core Ops, SparseCore 0:
  10.9 66.3 all-gather.4
  80.1 54.2 all-gather.6
  137.4 63.1 all-gather.8
  203.4 61.9 all-gather.10
  476.4 102.2 reduce-scatter.15
  584.5 98.5 reduce-scatter.9
  720.3 141.9 reduce-scatter.7
  868.8 135.0 reduce-scatter.13
  1010.4 135.0 reduce-scatter.11
where the time goes:
time: 1160 us
  matrix products  390 us (34%)
  waiting for transfers between devices  276 us (24%)
  blocking collectives  187 us (16%)
  other arithmetic  168 us (14%)
  local copies, waits for them, and re-layouts  82.2 us (7%)
  starting transfers between devices  28.1 us (2%)
  between operations  15.2 us (1%)
    reduce_scatter x1, waiting for transfers between devices, local(): lax.psum_scatter(grad_w_up, 'fsdp', scatter_dimension=0, tiled=True)  142 us
    unnamed x2, blocking collectives  140 us
    reduce_scatter x1, waiting for transfers between devices, local(): lax.psum_scatter(grad_w_down, 'fsdp', scatter_dimension=0, tiled=True)  132 us
    dot_general x2, matrix products, forward_pass(): jnp.dot(first_low, w_up, preferred_element_type=jnp.float32)  73.1 us
    sub x2, other arithmetic, attend(): exponent = jnp.exp(scores - row_max)  67.9 us
    dot_general x6, matrix products, masked_scores(): jnp.einsum('qhd,khd->hqk', query_block, keys_all, preferred_element_type=...  62.2 us
    convert_element_type x2, other arithmetic, attend_back(): grad_scores = (attn_probs * (grad_probs - jnp.sum(attn_probs * grad_probs...  44.7 us
    dot_general x4, matrix products, attend(): jnp.einsum('hqk,khd->qhd', attn_low, values_all, preferred_element_type=j...  40.4 us
  transfers between devices with their start and end apart: 12, of which 2 were waited for; matrix products, arithmetic and copies ran while one was open for 48% of the time, Pallas kernels for 0%

commit v1 on v0

v1 whole, which is shorter than its diff:
```python
from functools import partial

import jax
import jax.numpy as jnp
from jax import lax
from jax.experimental import pallas as pl
from jax.experimental.pallas import tpu as pltpu
from jax.sharding import PartitionSpec as P

HEADS = 12
HEAD_DIM = 64
AXIS = "fsdp"
MESH_ID = pl.DeviceIdType.MESH
VMEM_SPEC = pl.BlockSpec(memory_space=pltpu.VMEM)
ANY_SPEC = pl.BlockSpec(memory_space=pl.ANY)
VMEM_LIMIT = 60 * 1024 * 1024


def chain_edges(node, ring, lean_up):
    up_count = ring // 2 if lean_up else (ring - 1) // 2
    edges = []
    here = node
    for _ in range(up_count):
        there = ((here[0] + 1) % ring,) + here[1:]
        edges.append((here, there, "up"))
        here = there
    here = node
    for _ in range(ring - 1 - up_count):
        there = ((here[0] - 1) % ring,) + here[1:]
        edges.append((here, there, "down"))
        here = there
    return edges


def plane_edges(node, x_first):
    z = node[0]
    own, by_x, by_y, both = (z, 0, 0, 0), (z, 0, 1, 0), (z, 1, 0, 0), (z, 1, 1, 0)
    edges = [(own, by_x, "x"), (own, by_y, "y")]
    edges.append((by_x, both, "y") if x_first else (by_y, both, "x"))
    return edges


def make_tree(ring, ring_first, flip):
    root = (0, 0, 0, 0)
    edges = []
    if ring_first:
        edges += chain_edges(root, ring, flip)
        nodes = [root] + [edge[1] for edge in edges]
        for place, node in enumerate(nodes):
            edges += plane_edges(node, (place % 2 == 0) != flip)
    else:
        edges += plane_edges(root, flip)
        nodes = [root] + [edge[1] for edge in edges]
        for place, node in enumerate(nodes):
            edges += chain_edges(node, ring, (place % 2 == 0) != flip)
    nodes = [root] + [edge[1] for edge in edges]
    edges += [(node, node[:3] + (1,), "core") for node in nodes]
    depth = {root: 0}
    for parent, child, _ in edges:
        depth[child] = depth[parent] + 1
    order = sorted(range(len(edges)), key=lambda index: depth[edges[index][1]])
    return [edges[index] + (depth[edges[index][1]],) for index in order]


class Place:
    def __init__(self, ring):
        me = lax.axis_index(AXIS)
        self.ring = ring
        self.me = me
        self.core = lax.rem(me, 2)
        self.x = lax.rem(me // 2, 2)
        self.y = lax.rem(me // 4, 2)
        self.z = me // 8

    @staticmethod
    def flip(value, amount):
        return 1 - value if amount else value

    def chip_of(self, offset):
        z = lax.rem(self.z + (self.ring - offset[0]) % self.ring, self.ring)
        return (z * 2 + self.flip(self.y, offset[1])) * 2 + self.flip(self.x, offset[2])

    def unit_of(self, offset):
        return self.chip_of(offset) * 2 + self.flip(self.core, offset[3])

    def neighbour(self, way, back=False):
        step = {"up": (1, 0, 0, 0), "down": (-1, 0, 0, 0), "x": (0, 0, 1, 0)}
        step.update({"y": (0, 1, 0, 0), "core": (0, 0, 0, 1)})
        offset = step[way]
        dz = offset[0] if back else -offset[0]
        return self.unit_of((dz % self.ring,) + offset[1:])


def enter(place):
    barrier = pltpu.get_barrier_semaphore()
    for way in ("up", "down", "x", "y", "core"):
        pl.semaphore_signal(
            barrier, inc=1, device_id=(place.neighbour(way),), device_id_type=MESH_ID
        )
    pl.semaphore_wait(barrier, 5)


def gather_kernel(ring, plan, *refs):
    arrays = len(plan["shapes"])
    shards, outs = refs[:arrays], refs[arrays : 2 * arrays]
    recv_sem, send_sem, local_sem = refs[2 * arrays :]
    place = Place(ring)
    parts = plan["parts"]

    def window(ref, part):
        _, first, count, _ = parts[part]
        return ref if count is None else ref.at[pl.ds(first, count)]

    def copy(part, index):
        array, _, _, tree = parts[part]
        parent, _, way, _ = tree[index]
        unit = place.unit_of(parent)
        source = shards[array] if parent == (0, 0, 0, 0) else outs[array].at[unit]
        return pltpu.make_async_remote_copy(
            src_ref=window(source, part),
            dst_ref=window(outs[array].at[unit], part),
            send_sem=send_sem.at[part],
            recv_sem=recv_sem.at[part, index],
            device_id=(place.neighbour(way),),
            device_id_type=MESH_ID,
        )

    def arrived(part, index):
        array, _, _, tree = parts[part]
        _, child, way, _ = tree[index]
        landed = window(outs[array].at[place.unit_of(child)], part)
        pltpu.make_async_remote_copy(
            src_ref=landed,
            dst_ref=landed,
            send_sem=send_sem.at[part],
            recv_sem=recv_sem.at[part, index],
            device_id=(place.neighbour(way),),
            device_id_type=MESH_ID,
        ).wait_recv()

    def send_from(part, node):
        for index, edge in enumerate(parts[part][3]):
            if edge[0] == node:
                copy(part, index).start()

    own_copies = [
        pltpu.make_async_copy(shards[array], outs[array].at[place.me], local_sem.at[array])
        for array in range(arrays)
    ]
    for own_copy in own_copies:
        own_copy.start()
    enter(place)
    for part in range(len(parts)):
        send_from(part, (0, 0, 0, 0))
    deepest = max(edge[3] for part in parts for edge in part[3])
    for depth in range(1, deepest + 1):
        for part in range(len(parts)):
            for index, edge in enumerate(parts[part][3]):
                if edge[3] == depth and edge[2] != "core":
                    arrived(part, index)
                    send_from(part, edge[1])
    for part in range(len(parts)):
        for index, edge in enumerate(parts[part][3]):
            if edge[2] == "core":
                arrived(part, index)
    for own_copy in own_copies:
        own_copy.wait()
    for part, (array, first, count, tree) in enumerate(parts):
        whole = outs[array].at[pl.ds(0, len(tree))]
        if count is not None:
            whole = whole.at[:, pl.ds(first, count)]
        pltpu.make_async_copy(whole, whole, send_sem.at[part]).wait()


def gather_units(shards, plan, ring):
    devices = ring * 8
    edges = devices - 1
    return pl.pallas_call(
        partial(gather_kernel, ring, plan),
        out_shape=[
            jax.ShapeDtypeStruct((devices,) + shard.shape, shard.dtype) for shard in shards
        ],
        in_specs=[VMEM_SPEC] * len(shards),
        out_specs=[ANY_SPEC] * len(shards),
        scratch_shapes=[
            pltpu.SemaphoreType.DMA((len(plan["parts"]), edges)),
            pltpu.SemaphoreType.DMA((len(plan["parts"]),)),
            pltpu.SemaphoreType.DMA((len(shards),)),
        ],
        compiler_params=pltpu.CompilerParams(collective_id=0, has_side_effects=True),
        name="gather_units",
    )(*shards)


def scatter_kernel(ring, plan, *refs):
    shapes = plan["shapes"]
    arrays = len(shapes)
    parts = plan["parts"]
    grads, outs = refs[:arrays], refs[arrays : 2 * arrays]
    owns = refs[2 * arrays : 3 * arrays]
    lands = refs[3 * arrays : 3 * arrays + len(parts)]
    recv_sem, send_sem, local_sem = refs[3 * arrays + len(parts) :]
    place = Place(ring)

    def window(ref, part):
        _, first, count, _ = parts[part]
        return ref if count is None else ref.at[pl.ds(first, count)]

    def copy(part, index, source):
        way = parts[part][3][index][2]
        return pltpu.make_async_remote_copy(
            src_ref=source,
            dst_ref=lands[part].at[index],
            send_sem=send_sem.at[part],
            recv_sem=recv_sem.at[part, index],
            device_id=(place.neighbour(way, back=True),),
            device_id_type=MESH_ID,
        )

    own_copies = [
        pltpu.make_async_copy(grads[array].at[:, place.core], owns[array], local_sem.at[array])
        for array in range(arrays)
    ]
    for own_copy in own_copies:
        own_copy.start()
    enter(place)
    deepest = max(edge[3] for part in parts for edge in part[3])
    for depth in range(deepest, 0, -1):
        for part, (array, _, _, tree) in enumerate(parts):
            for index, (_, child, way, level) in enumerate(tree):
                if way == "core" and level == depth:
                    chip = place.chip_of(child)
                    source = grads[array].at[chip, place.flip(place.core, 1)]
                    copy(part, index, window(source, part)).start()
    for own_copy in own_copies:
        own_copy.wait()

    def add_up(part, node, target):
        array, first, count, tree = parts[part]
        children = [index for index, edge in enumerate(tree) if edge[0] == node]
        for index in children:
            copy(part, index, lands[part].at[index]).wait_recv()
        chip = place.chip_of(node)
        rows, columns = shapes[array]
        if count is not None:
            rows = count
        row_slice = pl.ds(first, rows)
        step = columns
        while rows * step > 24 * 768 and step % 256 == 0:
            step //= 2
        own = owns[array]

        def body(block, carry):
            where = pl.ds(pl.multiple_of(block * step, 128), step)
            total = own[chip, row_slice, where].astype(jnp.float32)
            for index in children:
                total = total + lands[part][index, :, where].astype(jnp.float32)
            if target is None:
                own[chip, row_slice, where] = total.astype(own.dtype)
            else:
                target[row_slice, where] = total
            return carry

        lax.fori_loop(0, columns // step, body, 0)
        return window(own.at[chip], part)

    waiting = None
    for depth in range(deepest, 0, -1):
        for part in range(len(parts)):
            for index, (_, child, way, level) in enumerate(parts[part][3]):
                if way != "core" and level == depth:
                    ready = copy(part, index, add_up(part, child, None))
                    if waiting is not None:
                        waiting.start()
                    waiting = ready
    waiting.start()
    for part in range(len(parts)):
        add_up(part, (0, 0, 0, 0), outs[parts[part][0]])
    for part in range(len(parts)):
        pltpu.make_async_copy(lands[part], lands[part], send_sem.at[part]).wait()


def scatter_units(grads, plan, ring):
    devices = ring * 8
    edges = devices - 1
    shapes = plan["shapes"]
    lands = []
    for array, _, count, _ in plan["parts"]:
        rows, columns = shapes[array]
        lands.append(
            pltpu.VMEM((edges, rows if count is None else count, columns), jnp.bfloat16)
        )
    return pl.pallas_call(
        partial(scatter_kernel, ring, plan),
        out_shape=[jax.ShapeDtypeStruct(shape, jnp.float32) for shape in shapes],
        in_specs=[ANY_SPEC] * len(shapes),
        out_specs=[VMEM_SPEC] * len(shapes),
        scratch_shapes=[pltpu.VMEM((devices // 2,) + shape, jnp.bfloat16) for shape in shapes]
        + lands
        + [
            pltpu.SemaphoreType.DMA((len(plan["parts"]), edges)),
            pltpu.SemaphoreType.DMA((len(plan["parts"]),)),
            pltpu.SemaphoreType.DMA((len(shapes),)),
        ],
        compiler_params=pltpu.CompilerParams(
            collective_id=1, has_side_effects=True, vmem_limit_bytes=VMEM_LIMIT
        ),
        name="scatter_units",
    )(*[grad.reshape((devices // 2, 2) + shape) for grad, shape in zip(grads, shapes)])


def make_plan(shapes, ring):
    ring_trees = [make_tree(ring, True, flip) for flip in (False, True)]
    plane_trees = [make_tree(ring, False, flip) for flip in (False, True)]
    order = [
        (0, None, plane_trees[0]),
        (1, None, plane_trees[1]),
        (2, None, ring_trees[0]),
        (3, 0, ring_trees[1]),
        (3, 1, plane_trees[1]),
        (4, None, ring_trees[1]),
    ]
    parts = []
    for array, piece, tree in order:
        half = shapes[array][0] // 2
        parts.append((array, (piece or 0) * half, None if piece is None else half, tree))
    return {"shapes": shapes, "parts": parts}


def masked_softmax(scores, inside_rows, inside_columns, diagonal):
    allowed = jnp.logical_or(jnp.logical_and(inside_rows, inside_columns), diagonal)
    scores = jnp.where(allowed, scores * 0.125, -1e30)
    exponent = jnp.exp(scores - jnp.max(scores, axis=-1, keepdims=True))
    return exponent, jnp.sum(exponent, axis=-1, keepdims=True)


def mask_parts(length, rows):
    row = lax.broadcasted_iota(jnp.int32, (rows, rows), 0)
    column = lax.broadcasted_iota(jnp.int32, (rows, rows), 1)
    return row < length, column < length, row == column


def dot_nt(left, right):
    return lax.dot_general(
        left, right, (((1,), (1,)), ((), ())), preferred_element_type=jnp.float32
    )


def dot_tn(left, right):
    return lax.dot_general(
        left, right, (((0,), (0,)), ((), ())), preferred_element_type=jnp.float32
    )


def dot_nn(left, right):
    return jnp.dot(left, right, preferred_element_type=jnp.float32)


def attend_kernel(lengths_ref, q_ref, k_ref, v_ref, context_ref):
    rows, width = q_ref.shape
    masks = mask_parts(lengths_ref[pl.program_id(0)], rows)
    lane = lax.broadcasted_iota(jnp.int32, (rows, width), 1)
    queries, keys, values = q_ref[...], k_ref[...], v_ref[...]
    context = jnp.zeros((rows, width), jnp.float32)
    for head in range(width // HEAD_DIM):
        mine = lane // HEAD_DIM == head
        scores = dot_nt(jnp.where(mine, queries, jnp.zeros_like(queries)), keys)
        exponent, total = masked_softmax(scores, *masks)
        probs = (exponent / total).astype(jnp.bfloat16)
        context = jnp.where(mine, dot_nn(probs, values), context)
    context_ref[...] = context.astype(context_ref.dtype)


def attend(qkv, lengths):
    rows, width3 = qkv.shape
    width = width3 // 3
    halves = lengths.shape[0]
    half = rows // halves
    pairs = width // 128

    def columns(which):
        return pl.BlockSpec((half, 128), lambda i, j, l: (i, which * pairs + j))

    return pl.pallas_call(
        attend_kernel,
        out_shape=jax.ShapeDtypeStruct((rows, width), jnp.bfloat16),
        grid_spec=pltpu.PrefetchScalarGridSpec(
            num_scalar_prefetch=1,
            grid=(halves, pairs),
            in_specs=[columns(0), columns(1), columns(2)],
            out_specs=columns(0),
        ),
        compiler_params=pltpu.CompilerParams(vmem_limit_bytes=VMEM_LIMIT),
        name="attend",
    )(lengths, qkv, qkv, qkv)


def attend_back_kernel(lengths_ref, q_ref, k_ref, v_ref, g_ref, grad_ref, sums_ref):
    rows, width = q_ref.shape
    masks = mask_parts(lengths_ref[pl.program_id(0)], rows)
    lane = lax.broadcasted_iota(jnp.int32, (rows, width), 1)
    queries, keys, values, grads = q_ref[...], k_ref[...], v_ref[...], g_ref[...]
    zero = jnp.zeros_like(queries)
    grad_q = jnp.zeros((rows, width), jnp.float32)
    grad_k, grad_v = grad_q, grad_q
    for head in range(width // HEAD_DIM):
        mine = lane // HEAD_DIM == head
        scores = dot_nt(jnp.where(mine, queries, zero), keys)
        exponent, total = masked_softmax(scores, *masks)
        probs = exponent / total
        grad_v = jnp.where(mine, dot_tn(probs.astype(jnp.bfloat16), grads), grad_v)
        grad_probs = dot_nt(jnp.where(mine, grads, zero), values)
        along = jnp.sum(probs * grad_probs, axis=-1, keepdims=True)
        grad_scores = (probs * (grad_probs - along)).astype(jnp.bfloat16)
        grad_q = jnp.where(mine, dot_nn(grad_scores, keys) * 0.125, grad_q)
        grad_k = jnp.where(mine, dot_tn(grad_scores, queries) * 0.125, grad_k)
    for place, grad in enumerate((grad_q, grad_k, grad_v)):
        grad_ref[place] = grad.astype(grad_ref.dtype)
        sums_ref[0, place] = jnp.sum(grad, axis=0, keepdims=True)


def attend_back(qkv, grad_context, lengths):
    rows, width3 = qkv.shape
    width = width3 // 3
    halves = lengths.shape[0]
    half = rows // halves
    pairs = width // 128

    def columns(which):
        return pl.BlockSpec((half, 128), lambda i, j, l: (i, which * pairs + j))

    return pl.pallas_call(
        attend_back_kernel,
        out_shape=[
            jax.ShapeDtypeStruct((3, rows, width), jnp.bfloat16),
            jax.ShapeDtypeStruct((halves, 3, 1, width), jnp.float32),
        ],
        grid_spec=pltpu.PrefetchScalarGridSpec(
            num_scalar_prefetch=1,
            grid=(halves, pairs),
            in_specs=[columns(0), columns(1), columns(2), columns(0)],
            out_specs=[
                pl.BlockSpec((3, half, 128), lambda i, j, l: (0, i, j)),
                pl.BlockSpec((1, 3, 1, 128), lambda i, j, l: (i, 0, 0, j)),
            ],
        ),
        compiler_params=pltpu.CompilerParams(vmem_limit_bytes=VMEM_LIMIT),
        name="attend_back",
    )(lengths, qkv, qkv, qkv, grad_context)


ERFC_TERMS = (
    0.17087277,
    -0.82215223,
    1.48851587,
    -1.13520398,
    0.27886807,
    -0.18628806,
    0.09678418,
    0.37409196,
    1.00002368,
    -1.26551223,
)


def gelu_parts(u):
    x = jnp.abs(u) * 0.7071067811865476
    square = -0.5 * u * u
    t = 1.0 / (1.0 + 0.5 * x)
    poly = ERFC_TERMS[0]
    for term in ERFC_TERMS[1:]:
        poly = poly * t + term
    tail = 0.5 * t * jnp.exp(poly + square)
    cdf = jnp.where(u < 0, tail, 1.0 - tail)
    return u * cdf, cdf + u * jnp.exp(square) * 0.3989422804014327


def up_kernel(first_ref, w_ref, b_ref, active_ref, slope_ref):
    rows = first_ref.shape[0]
    step = 128
    for start in range(0, rows, step):
        where = pl.ds(start, step)
        u = dot_nn(first_ref[where, :], w_ref[...]) + b_ref[...]
        value, slope = gelu_parts(u)
        active_ref[where, :] = value.astype(active_ref.dtype)
        slope_ref[where, :] = slope.astype(slope_ref.dtype)


def up_project(first_low, w_up, b_up):
    rows, width = first_low.shape
    hidden = w_up.shape[1]
    block = 512
    return pl.pallas_call(
        up_kernel,
        out_shape=[jax.ShapeDtypeStruct((rows, hidden), jnp.bfloat16)] * 2,
        grid=(hidden // block,),
        in_specs=[
            pl.BlockSpec((rows, width), lambda j: (0, 0)),
            pl.BlockSpec((width, block), lambda j: (0, j)),
            pl.BlockSpec((1, block), lambda j: (0, j)),
        ],
        out_specs=[pl.BlockSpec((rows, block), lambda j: (0, j))] * 2,
        compiler_params=pltpu.CompilerParams(vmem_limit_bytes=VMEM_LIMIT),
        name="up_project",
    )(first_low, w_up, b_up.reshape(1, hidden))


def norm_parts(hidden):
    center = hidden - jnp.mean(hidden, axis=-1, keepdims=True)
    inverse = lax.rsqrt(jnp.mean(center * center, axis=-1, keepdims=True) + 1e-12)
    return (center * inverse, inverse)


def norm_back(grad_out, normed, inverse, gain):
    scaled = grad_out * gain
    centered = scaled - jnp.mean(scaled, axis=-1, keepdims=True)
    return inverse * (centered - normed * jnp.mean(scaled * normed, axis=-1, keepdims=True))


def block_slots(lengths, row_count):
    half = row_count // 2
    row = jnp.arange(row_count, dtype=jnp.int32)
    first, second = lengths[0], lengths[1]
    slot = jnp.where(
        row < half,
        jnp.where(row < first, row, row + second),
        jnp.where(row - half < second, row - half + first, row),
    )
    return slot, jnp.where(row < half, row < first, row - half < second)


def gather_params(params, ring):
    (w_qkv, b_qv, w_out, b_out, g1, c1, w_up, b_up, w_down, b_down, g2, c2, w_proj) = params
    small = [b_qv, b_out, g1, c1, b_up, b_down, g2, c2]
    sizes = [entry.shape[0] for entry in small]
    if ring is None:
        whole = [lax.all_gather(w, AXIS, axis=0, tiled=True) for w in (w_qkv, w_out, w_up, w_down)]
        proj = lax.all_gather(w_proj, AXIS, axis=0, tiled=True)
        few = lax.all_gather(jnp.concatenate(small), AXIS, axis=0)
    else:
        packed = jnp.concatenate(small)
        packed = jnp.pad(packed, (0, 1024 - packed.shape[0])).reshape(8, 128)
        shards = [w_qkv, w_out, w_up, w_down, jnp.concatenate([w_proj, packed], axis=0)]
        plan = make_plan([shard.shape for shard in shards], ring)
        units = gather_units(shards, plan, ring)
        whole = [unit.reshape(-1, unit.shape[2]) for unit in units[:4]]
        rows = w_proj.shape[0]
        proj = units[4][:, :rows].reshape(-1, w_proj.shape[1])
        few = units[4][:, rows:].reshape(units[4].shape[0], -1)
    vectors = []
    start = 0
    for size in sizes:
        vectors.append(few[:, start : start + size].reshape(-1).astype(jnp.float32))
        start += size
    return whole + [proj], vectors


def scatter_grads(weights, vectors, ring, devices):
    few = [vector.reshape(devices, -1) for vector in vectors]
    sizes = [entry.shape[1] for entry in few]
    few = jnp.concatenate(few, axis=1)
    if ring is None:
        shards = [
            lax.psum_scatter(w, AXIS, scatter_dimension=0, tiled=True).astype(jnp.float32)
            for w in weights
        ]
        small = lax.psum_scatter(few.reshape(-1), AXIS, scatter_dimension=0, tiled=True)
    else:
        few = jnp.pad(few, ((0, 0), (0, 1024 - few.shape[1]))).astype(jnp.bfloat16)
        units = [w.reshape(devices, -1, w.shape[1]) for w in weights]
        rows = units[4].shape[1]
        units[4] = jnp.concatenate([units[4], few.reshape(devices, 8, 128)], axis=1)
        plan = make_plan([unit.shape[1:] for unit in units], ring)
        shards = list(scatter_units(units, plan, ring))
        small = shards[4][rows:].reshape(-1)
        shards[4] = shards[4][:rows]
    pieces = []
    start = 0
    for size in sizes:
        pieces.append(small[start : start + size])
        start += size
    return shards, pieces


def local(tokens, cotangent, slot_row, lengths, *params):
    devices = lax.axis_size(AXIS)
    row_count, model_width = tokens.shape
    peer_rows = row_count // devices
    ring = devices // 8 if params[0].shape[0] % 8 == 0 and devices % 8 == 0 else None
    (w_qkv, w_out, w_up, w_down, w_proj), vectors = gather_params(params, ring)
    b_qv, b_out, gain_one, bias_one, b_up, b_down, gain_two, bias_two = vectors

    slot, inside = block_slots(lengths, row_count)
    local_row = (slot_row // row_count * peer_rows + slot_row % peer_rows)[slot]
    both = jnp.concatenate([tokens, cotangent], axis=1)
    arrived = lax.all_to_all(both, AXIS, split_axis=0, concat_axis=0, tiled=True)[local_row]
    dealt, dealt_cot = arrived[:, :model_width], arrived[:, model_width:]
    valid = inside[:, None].astype(jnp.float32)

    bias_all = jnp.concatenate(
        [b_qv[:model_width], jnp.zeros((model_width,), jnp.float32), b_qv[model_width:]]
    )
    qkv = (dot_nn(dealt, w_qkv) + bias_all).astype(jnp.bfloat16)
    context = attend(qkv, lengths)
    hidden_one = dealt.astype(jnp.float32) + dot_nn(context, w_out) + b_out
    normed_one, inverse_one = norm_parts(hidden_one)
    first_low = (normed_one * gain_one + bias_one).astype(jnp.bfloat16)
    active, slope = up_project(first_low, w_up, b_up)
    hidden_two = first_low.astype(jnp.float32) + dot_nn(active, w_down) + b_down
    normed_two, inverse_two = norm_parts(hidden_two)
    second_low = (normed_two * gain_two + bias_two).astype(jnp.bfloat16)
    project = dot_nn(second_low, w_proj)
    inv_norm = lax.rsqrt(jnp.sum(project * project, axis=-1, keepdims=True) + 1e-06)
    embedded = (project * inv_norm * valid).astype(jnp.bfloat16)

    grad_emb = dealt_cot.astype(jnp.float32) * valid
    along = jnp.sum(project * grad_emb, axis=-1, keepdims=True)
    grad_project = (inv_norm * grad_emb - inv_norm * inv_norm * inv_norm * along * project).astype(
        jnp.bfloat16
    )
    grad_w_proj = dot_tn(second_low, grad_project).astype(jnp.bfloat16)
    grad_second = dot_nt(grad_project, w_proj)
    grad_gain_two = jnp.sum(grad_second * normed_two, axis=0)
    grad_bias_two = jnp.sum(grad_second, axis=0)
    grad_hidden_two = norm_back(grad_second, normed_two, inverse_two, gain_two)
    grad_b_down = jnp.sum(grad_hidden_two, axis=0)
    down_low = grad_hidden_two.astype(jnp.bfloat16)
    grad_w_down = dot_tn(active, down_low).astype(jnp.bfloat16)
    grad_up = dot_nt(down_low, w_down) * slope.astype(jnp.float32)
    grad_b_up = jnp.sum(grad_up, axis=0)
    up_low = grad_up.astype(jnp.bfloat16)
    grad_w_up = dot_tn(first_low, up_low).astype(jnp.bfloat16)
    grad_first = grad_hidden_two + dot_nt(up_low, w_up)
    grad_gain_one = jnp.sum(grad_first * normed_one, axis=0)
    grad_bias_one = jnp.sum(grad_first, axis=0)
    grad_hidden_one = norm_back(grad_first, normed_one, inverse_one, gain_one)
    grad_b_out = jnp.sum(grad_hidden_one, axis=0)
    out_low = grad_hidden_one.astype(jnp.bfloat16)
    grad_w_out = dot_tn(context, out_low).astype(jnp.bfloat16)
    grad_context = dot_nt(out_low, w_out).astype(jnp.bfloat16)
    grad_three, sums = attend_back(qkv, grad_context, lengths)
    sums = jnp.sum(sums, axis=0)[:, 0]
    grad_b_qv = jnp.concatenate([sums[0], sums[2]])
    grad_qkv = jnp.concatenate([grad_three[0], grad_three[1], grad_three[2]], axis=1)
    grad_w_qkv = dot_tn(dealt, grad_qkv).astype(jnp.bfloat16)
    grad_dealt = (dot_nt(grad_qkv, w_qkv) + grad_hidden_one).astype(jnp.bfloat16)

    inverse_row = (
        jnp.zeros((row_count,), jnp.int32).at[local_row].set(jnp.arange(row_count, dtype=jnp.int32))
    )
    back = jnp.concatenate([grad_dealt, embedded], axis=1)[inverse_row]
    returned = lax.all_to_all(back, AXIS, split_axis=0, concat_axis=0, tiled=True)
    shards, small = scatter_grads(
        [grad_w_qkv, grad_w_out, grad_w_up, grad_w_down, grad_w_proj],
        [
            grad_b_qv,
            grad_b_out,
            grad_gain_one,
            grad_bias_one,
            grad_b_up,
            grad_b_down,
            grad_gain_two,
            grad_bias_two,
        ],
        ring,
        devices,
    )
    return (
        returned[:, model_width:],
        returned[:, :model_width],
        shards[0],
        small[0],
        shards[1],
        small[1],
        small[2],
        small[3],
        shards[2],
        small[4],
        shards[3],
        small[5],
        small[6],
        small[7],
        shards[4],
    )


def solution(mesh):
    matrix, vector = P(AXIS, None), P(AXIS)
    params = "mvmvvvmvmvvvm"
    in_kinds = "mmvv" + params
    out_kinds = "mm" + params
    specs = {"m": matrix, "v": vector}
    return jax.shard_map(
        local,
        mesh=mesh,
        in_specs=tuple(specs[kind] for kind in in_kinds),
        out_specs=tuple(specs[kind] for kind in out_kinds),
        check_vma=False,
    )
```

time: 1160 us -> 456 us (0.39)
  matrix products: 390 us -> 89.6 us
  Pallas kernels: 0 us -> 284 us
  waiting for transfers between devices: 276 us -> 0.01 us
  blocking collectives: 187 us -> 0 us
  other arithmetic: 168 us -> 20.5 us
  local copies, waits for them, and re-layouts: 82.2 us -> 41.1 us
  starting transfers between devices: 28.1 us -> 11.2 us
  between operations: 15.2 us -> 1.5 us
    dot_general x37 -> x14, matrix products: 390 us -> 89.6 us  [the longest x5 34.7 us: dot_tn(): lax.dot_general(left, right, (((0,), (0,)), ((), ())), preferred_element_...]
    pallas_call x0 -> x5, Pallas kernels: none -> 284 us  [the longest x1 117 us: gather_units(): pl.pallas_call(partial(gather_kernel, ring, plan), out_shape=[jax.ShapeDt...]
    reduce_scatter x4 -> x0, waiting for transfers between devices: 273 us -> none  [the longest x1 142 us: local(): lax.psum_scatter(grad_w_up, 'fsdp', scatter_dimension=0, tiled=True)]
    unnamed x2 -> x0, blocking collectives: 140 us -> none
    sub x2 -> x0, other arithmetic: 67.9 us -> none  [attend(): exponent = jnp.exp(scores - row_max)]
    convert_element_type x13 -> x7, other arithmetic: 50.8 us -> 6.02 us  [the longest x1 2.27 us: local(): (inv_norm * grad_emb - inv_norm * inv_norm * inv_norm * along * project)....]
    reduce_sum x8 -> x4, other arithmetic: 38.8 us -> 5.79 us  [the longest x1 3 us: local(): grad_b_out = jnp.sum(grad_hidden_one, axis=0)]
    all_gather x1 -> x0, blocking collectives: 32.8 us -> none  [local(): lax.all_gather(w_proj, 'fsdp', axis=0, tiled=True)]
  transfers between devices with their start and end apart: 12 -> 2, of which waited for: 2 -> 0; matrix products, arithmetic and copies ran while one was open for 48% -> 10% of each run, Pallas kernels for 0% -> 47%
where the time goes in v1:
time: 456 us; the launch traced here: 448 us
  Pallas kernels  284 us (62%)
  matrix products  89.6 us (20%)
  local copies, waits for them, and re-layouts  41.1 us (9%)
  other arithmetic  20.5 us (4%)
  starting transfers between devices  11.2 us (2%)
    pallas_call x1, Pallas kernels, gather_units(): pl.pallas_call(partial(gather_kernel, ring, plan), out_shape=[jax.ShapeDt...  117 us
    pallas_call x1, Pallas kernels, scatter_units(): pl.pallas_call(partial(scatter_kernel, ring, plan), out_shape=[jax.ShapeD...  91.4 us
    dot_general x5, matrix products, dot_tn(): lax.dot_general(left, right, (((0,), (0,)), ((), ())), preferred_element_...  34.7 us
    pallas_call x1, Pallas kernels, attend_back(): pl.pallas_call(attend_back_kernel, out_shape=[jax.ShapeDtypeStruct((3, ro...  33.7 us
    dot_general x5, matrix products, dot_nt(): lax.dot_general(left, right, (((1,), (1,)), ((), ())), preferred_element_...  32.1 us
    dot_general x4, matrix products, dot_nn(): return jnp.dot(left, right, preferred_element_type=jnp.float32)  22.8 us
    pallas_call x1, Pallas kernels, up_project(): pl.pallas_call(up_kernel, out_shape=[jax.ShapeDtypeStruct((rows, hidden),...  22.3 us
    pallas_call x1, Pallas kernels, attend(): pl.pallas_call(attend_kernel, out_shape=jax.ShapeDtypeStruct((rows, width...  19.5 us
  transfers between devices with their start and end apart: 2, of which 0 were waited for; matrix products, arithmetic and copies ran while one was open for 10% of the time, Pallas kernels for 47%

profile of v1, /device:TPU:18, one launch (start us, length us, event | category | flops | bytes accessed | tf_op | source)
XLA Modules:
  0.0 448.0 jit_solution(120910497555806509)
XLA Ops:
  0.7 2.9 pad_maximum_fusion.3
  3.7 5.9 %all-to-all-start = ((bf16[32,32,896]{2,1,0:T(8,128)(2,1)}), bf16[32,32,896]{2,1,0:T(8,128)(2,1)S(1)}, u32[]{:S(2)}, u32[]{:S(2)}) async-start(bf16[32,32,896]{2,1,0:T(8,128)(2,1)} %bitcast.58), calls=%async_computation | async-start | bytes 3670016 | tf_op jit(solution)/shard_map/all_to_all | solution.py:596
  10.4 117.3 %gather_units.1 = (bf16[32,24,2304]{2,1,0:T(8,128)(2,1)}, bf16[32,24,768]{2,1,0:T(8,128)(2,1)}, bf16[32,24,3072]{2,1,0:T(8,128)(2,1)}, bf16[32,96,768]{2,1,0:T(8,128)(2,1)}, bf16[32,32,128]{2,1,0:T(8,128)(2,1)}) custom-call(bf16[24,2304]{1,0:T(8,128)(2,1)} %refs_0_.1, bf16[24,768]{1,0:T(8,128)(2,1)} %refs_1_.1, bf16[24,3072]{1,0:T(8,128)(2,1)} %refs_2_.1, ...), custom_call_target="tpu_custom_call" | custom-call | tf_op jit(solution)/shard_map/gather_units/pallas_call | solution.py:178
  133.0 4.5 %gather_fusion = s32[1024]{0:T(1024)S(1)} fusion(s32[1024]{0:T(1024)S(1)} %get-tuple-element.90, s32[1024]{0:T(1024)S(1)} %get-tuple-element.91), kind=kCustom, calls=%fused_computation | custom fusion | bytes 12288 | tf_op jit(solution)/shard_map/gather | solution.py:594
  137.5 4.5 %scatter_custom_fusion = s32[1024]{0:T(1024)S(1)} fusion(s32[1024]{0:T(1024)S(1)} %bitcast.77, s32[1024]{0:T(1024)S(1)} %iota.36, s32[]{:T(128)} %constant.46.clone.1), kind=kCustom, calls=%fused_computation.106 | custom fusion | bytes 4100 | tf_op jit(solution)/shard_map/scatter | solution.py:649
  143.4 5.3 %gather_fusion.1 = bf16[1024,896]{1,0:T(8,128)(2,1)} fusion(bf16[1024,896]{1,0:T(8,128)(2,1)S(1)} %bitcast.56, s32[1024]{0:T(1024)S(1)} %broadcast_clamp_fusion.1), kind=kCustom, calls=%fused_computation.1 | custom fusion | bytes 3674112 | tf_op jit(solution)/shard_map/gather | solution.py:596
  148.7 8.5 %add_convert_fusion.q_ref.k_ref.v_ref = bf16[1024,2304]{1,0:T(8,128)(2,1)} fusion(bf16[768,2304]{1,0:T(8,128)(2,1)} %bitcast.83, f32[2304]{0:T(1024)S(1)} %pad_maximum_fusion.8, bf16[1024,896]{1,0:T(8,128)(2,1)} %gather_fusion.1), kind=kOutput, calls=%fused_computation.5 | convolution fusion | flops 3628597248 | bytes 9839616 | tf_op jit(solution)/shard_map/dot_general | solution.py:356
  157.1 19.5 %attend.1 = bf16[1024,768]{1,0:T(8,128)(2,1)} custom-call(s32[2]{0:T(128)} %lengths_ref.3, bf16[1024,2304]{1,0:T(8,128)(2,1)} %add_convert_fusion.q_ref.k_ref.v_ref, bf16[1024,2304]{1,0:T(8,128)(2,1)} %add_convert_fusion.q_ref.k_ref.v_ref, bf16[1024,2304]{1,0:T(8,128)(2,1)} %add_convert_fusion.q_ref.k_ref.v_ref), custom_call_target="tpu_custom_call" | custom-call | tf_op jit(solution)/shard_map/attend/pallas_call | solution.py:384
  176.6 3.8 fusion.30
  182.6 22.3 %up_project.1 = (bf16[1024,3072]{1,0:T(8,128)(2,1)}, bf16[1024,3072]{1,0:T(8,128)(2,1)}) custom-call(bf16[1024,768]{1,0:T(8,128)(2,1)} %add_convert_fusion.3.first_ref, bf16[768,3072]{1,0:T(8,128)(2,1)} %bitcast.63, f32[1,3072]{1,0:T(1,128)} %reshape.323.b_ref), custom_call_target="tpu_custom_call" | custom-call | tf_op jit(solution)/shard_map/up_project/pallas_call | solution.py:493
  204.9 9.1 %fusion.31 = (f32[1024]{0:T(1024)S(1)}, f32[1024,768]{1,0:T(8,128)S(1)}) fusion(f32[768]{0:T(1024)S(1)} %reshape.324, bf16[1024,3072]{1,0:T(8,128)(2,1)} %get-tuple-element.33, bf16[3072,768]{1,0:T(8,128)(2,1)} %bitcast.81, bf16[1024,768]{1,0:T(8,128)(2,1)} %add_convert_fusion.3.first_ref), kind=kOutput, calls=%fused_computation.116 | convolution fusion | flops 4834982912 | bytes 15735808 | tf_op jit(solution)/shard_map/dot_general | solution.py:356
  224.3 2.7 convolution_convert_fusion.5
  229.6 12.6 %fusion = (bf16[3072]{0:T(1024)(128)(2,1)S(1)}, f32[1024,3072]{1,0:T(8,128)}) fusion(bf16[1024,3072]{1,0:T(8,128)(2,1)} %get-tuple-element.35, bf16[3072,768]{1,0:T(8,128)(2,1)} %bitcast.82, f32[1024,768]{1,0:T(8,128)S(1)} %get-tuple-element.54), kind=kOutput, calls=%fused_computation.6 | convolution fusion | flops 4842058752 | bytes 26744832 | tf_op jit(solution)/shard_map/dot_general | solution.py:344
  242.2 11.7 %multiply_reduce_fusion.1 = (bf16[768]{0:T(1024)(128)(2,1)S(1)}, f32[1024]{0:T(1024)S(1)}, f32[1024]{0:T(1024)S(1)}, bf16[768]{0:T(1024)(128)(2,1)S(1)}, f32[1024,768]{1,0:T(8,128)}) fusion(f32[1024,768]{1,0:T(8,128)S(1)} %get-tuple-element.81, f32[1024]{0:T(1024)S(1)} %add_rsqrt_fusion.2, f32[1024]{0:T(1024)S(1)} %broadcast_multiply_fusion.5, ...), kind=kOutput, calls=%fused_computation.13 | convolution fusion | flops 4849135616 | bytes 33052672 | tf_op jit(solution)/shard_map/dot_general | solution.py:344
  253.9 3.0 fusion.26
  262.1 33.7 %attend_back.1 = (bf16[3,1024,768]{2,1,0:T(8,128)(2,1)}, f32[2,3,1,768]{3,2,1,0:T(1,128)}) custom-call(s32[2]{0:T(128)} %lengths_ref.3, bf16[1024,2304]{1,0:T(8,128)(2,1)} %add_convert_fusion.q_ref.k_ref.v_ref, bf16[1024,2304]{1,0:T(8,128)(2,1)} %add_convert_fusion.q_ref.k_ref.v_ref, bf16[1024,2304]{1,0:T(8,128)(2,1)} %add_convert_fusion.q_ref.k_ref.v_ref, ...), custom_call_target="tpu_custom_call" | custom-call | tf_op jit(solution)/shard_map/attend_back/pallas_call | solution.py:432
  295.8 2.8 slice_bitcast_fusion.2
  300.1 3.9 add_convert_fusion.1
  304.0 6.1 %convolution_convert_fusion.2 = bf16[768,2304]{1,0:T(8,128)(2,1)} fusion(bf16[1024,768]{1,0:T(8,128)(2,1)S(1)} %get-tuple-element.58, bf16[1024,768]{1,0:T(8,128)(2,1)S(1)} %get-tuple-element.59, bf16[1024,768]{1,0:T(8,128)(2,1)S(1)} %get-tuple-element.57, bf16[1024,896]{1,0:T(8,128)(2,1)S(1)} %copy-done.8), kind=kOutput, calls=%fused_computation.10 | convolution fusion | flops 3639803904 | bytes 9830400 | tf_op jit(solution)/shard_map/dot_general | solution.py:350
  312.1 5.3 %gather_fusion.2 = bf16[1024,896]{1,0:T(8,128)(2,1)} fusion(bf16[1024,896]{1,0:T(8,128)(2,1)S(1)} %pad_maximum_fusion.4, s32[1024]{0:T(1024)S(1)} %fusion.14), kind=kCustom, calls=%fused_computation.2 | custom fusion | bytes 3674112 | tf_op jit(solution)/shard_map/gather | solution.py:651
  317.4 5.3 %all-to-all-start.1 = ((bf16[32,32,896]{2,1,0:T(8,128)(2,1)}), bf16[32,32,896]{2,1,0:T(8,128)(2,1)S(1)}, u32[]{:S(2)}, u32[]{:S(2)}) async-start(bf16[32,32,896]{2,1,0:T(8,128)(2,1)} %bitcast.57), calls=%async_computation.1 | async-start | bytes 3670016 | tf_op jit(solution)/shard_map/all_to_all | solution.py:652
  324.5 13.5 %convolution_convert_fusion.1 = bf16[768,3072]{1,0:T(8,128)(2,1)} fusion(bf16[1024,768]{1,0:T(8,128)(2,1)S(1)} %copy-done.3, f32[1024,3072]{1,0:T(8,128)} %get-tuple-element.89, bf16[1024,3072]{1,0:T(8,128)(2,1)} %get-tuple-element.35), kind=kOutput, calls=%fused_computation.9 | convolution fusion | flops 4843634688 | bytes 25165824 | tf_op jit(solution)/shard_map/dot_general | solution.py:350
  338.1 9.9 %convolution_convert_fusion = bf16[3072,768]{1,0:T(8,128)(2,1)} fusion(bf16[1024,3072]{1,0:T(8,128)(2,1)} %get-tuple-element.33, f32[1024,768]{1,0:T(8,128)S(1)} %copy-done.5), kind=kOutput, calls=%fused_computation.8 | convolution fusion | flops 4834983936 | bytes 14155776 | tf_op jit(solution)/shard_map/dot_general | solution.py:350
  347.9 91.4 %scatter_units.1 = (f32[24,2304]{1,0:T(8,128)}, f32[24,768]{1,0:T(8,128)}, f32[24,3072]{1,0:T(8,128)}, f32[96,768]{1,0:T(8,128)}, f32[32,128]{1,0:T(8,128)}) custom-call(bf16[16,2,24,2304]{3,2,1,0:T(8,128)(2,1)} %bitcast.67, bf16[16,2,24,768]{3,2,1,0:T(8,128)(2,1)} %bitcast.68, bf16[16,2,24,3072]{3,2,1,0:T(8,128)(2,1)} %bitcast.61, ...), custom_call_target="tpu_custom_call" | custom-call | tf_op jit(solution)/shard_map/scatter_units/pallas_call | solution.py:293
  (141 shorter events, 41.2 us)
Async XLA Ops:
  0.6 9.0 %copy-start.25 = (bf16[24]{0:T(256)(128)(2,1)S(1)}, bf16[24]{0:T(256)(128)(2,1)}, u32[]{:S(2)}) copy-start(bf16[24]{0:T(256)(128)(2,1)} %param.32) | copy-start | bytes 148
  0.7 9.0 %copy-start.24 = (bf16[24]{0:T(256)(128)(2,1)S(1)}, bf16[24]{0:T(256)(128)(2,1)}, u32[]{:S(2)}) copy-start(bf16[24]{0:T(256)(128)(2,1)} %param.31) | copy-start | bytes 148
  0.7 9.0 %copy-start.23 = (bf16[24]{0:T(256)(128)(2,1)S(1)}, bf16[24]{0:T(256)(128)(2,1)}, u32[]{:S(2)}) copy-start(bf16[24]{0:T(256)(128)(2,1)} %param.30) | copy-start | bytes 148
  0.7 9.0 %copy-start.22 = (bf16[96]{0:T(256)(128)(2,1)S(1)}, bf16[96]{0:T(256)(128)(2,1)}, u32[]{:S(2)}) copy-start(bf16[96]{0:T(256)(128)(2,1)} %param.28) | copy-start | bytes 580
  0.7 9.0 %copy-start.21 = (bf16[24]{0:T(256)(128)(2,1)S(1)}, bf16[24]{0:T(256)(128)(2,1)}, u32[]{:S(2)}) copy-start(bf16[24]{0:T(256)(128)(2,1)} %param.26) | copy-start | bytes 148
  0.7 9.0 %copy-start.20 = (bf16[24]{0:T(256)(128)(2,1)S(1)}, bf16[24]{0:T(256)(128)(2,1)}, u32[]{:S(2)}) copy-start(bf16[24]{0:T(256)(128)(2,1)} %param.25) | copy-start | bytes 148
  0.7 9.0 %copy-start.19 = (bf16[24]{0:T(256)(128)(2,1)S(1)}, bf16[24]{0:T(256)(128)(2,1)}, u32[]{:S(2)}) copy-start(bf16[24]{0:T(256)(128)(2,1)} %param.24) | copy-start | bytes 148
  0.7 9.0 %copy-start.18 = (bf16[48]{0:T(256)(128)(2,1)S(1)}, bf16[48]{0:T(256)(128)(2,1)}, u32[]{:S(2)}) copy-start(bf16[48]{0:T(256)(128)(2,1)} %param.22) | copy-start | bytes 292
  0.7 9.1 %copy-start.16 = (bf16[24,128]{1,0:T(8,128)(2,1)S(1)}, bf16[24,128]{1,0:T(8,128)(2,1)}, u32[]{:S(2)}) copy-start(bf16[24,128]{1,0:T(8,128)(2,1)} %param.33) | copy-start | bytes 18436
  3.7 127.4 %copy-start.15 = (s32[2]{0:T(128)S(1)}, s32[2]{0:T(128)}, u32[]{:S(2)}) copy-start(s32[2]{0:T(128)} %lengths_ref.3) | copy-start | bytes 28
  3.7 129.3 %copy-start.17 = (s32[1024]{0:T(1024)S(1)}, s32[1024]{0:T(1024)}, u32[]{:S(2)}) copy-start(s32[1024]{0:T(1024)} %param.19) | copy-start | bytes 12292
  3.7 139.7 %all-to-all-start = ((bf16[32,32,896]{2,1,0:T(8,128)(2,1)}), bf16[32,32,896]{2,1,0:T(8,128)(2,1)S(1)}, u32[]{:S(2)}, u32[]{:S(2)}) async-start(bf16[32,32,896]{2,1,0:T(8,128)(2,1)} %bitcast.58), calls=%async_computation | async-start | bytes 3670016 | tf_op jit(solution)/shard_map/all_to_all | solution.py:596
  220.4 6.6 %copy-start.1 = (f32[1024,768]{1,0:T(8,128)S(1)}, f32[1024,768]{1,0:T(8,128)}, u32[]{:S(2)}) copy-start(f32[1024,768]{1,0:T(8,128)} %copy-done) | copy-start | bytes 9437188
  228.5 13.7 %slice-start = ((s8[4718592]{0:T(1024)(128)(4,1)}), s8[4194304]{0:T(1024)(128)(4,1)S(1)}, s32[]{:S(2)}) async-start(s8[4718592]{0:T(1024)(128)(4,1)} %bitcast.64), calls=%async_computation.2 | async-start | bytes 8388608
  229.6 12.6 %copy-start.4 = (f32[1024,768]{1,0:T(8,128)}, f32[1024,768]{1,0:T(8,128)S(1)}, u32[]{:S(2)}) copy-start(f32[1024,768]{1,0:T(8,128)S(1)} %get-tuple-element.54) | copy-start | bytes 9437188
  229.6 12.6 %slice-start.1 = ((s8[4718592]{0:T(1024)(128)(4,1)}), s8[524288]{0:T(1024)(128)(4,1)S(1)}, s32[]{:S(2)}) async-start(s8[4718592]{0:T(1024)(128)(4,1)} %bitcast.64), calls=%async_computation.3 | async-start | bytes 1048576
  304.0 6.8 %copy-start.14 = (f32[2,3,1,768]{3,2,1,0:T(1,128)S(1)}, f32[2,3,1,768]{3,2,1,0:T(1,128)}, u32[]{:S(2)}) copy-start(f32[2,3,1,768]{3,2,1,0:T(1,128)} %get-tuple-element.37) | copy-start | bytes 55300
  317.4 7.1 %copy-start.3 = (bf16[1024,768]{1,0:T(8,128)(2,1)S(1)}, bf16[1024,768]{1,0:T(8,128)(2,1)}, u32[]{:S(2)}) copy-start(bf16[1024,768]{1,0:T(8,128)(2,1)} %add_convert_fusion.3.first_ref) | copy-start | bytes 4718596
  317.4 125.7 %all-to-all-start.1 = ((bf16[32,32,896]{2,1,0:T(8,128)(2,1)}), bf16[32,32,896]{2,1,0:T(8,128)(2,1)S(1)}, u32[]{:S(2)}, u32[]{:S(2)}) async-start(bf16[32,32,896]{2,1,0:T(8,128)(2,1)} %bitcast.57), calls=%async_computation.1 | async-start | bytes 3670016 | tf_op jit(solution)/shard_map/all_to_all | solution.py:652
  324.5 13.5 %copy-start.5 = (f32[1024,768]{1,0:T(8,128)S(1)}, f32[1024,768]{1,0:T(8,128)}, u32[]{:S(2)}) copy-start(f32[1024,768]{1,0:T(8,128)} %copy-done.4) | copy-start | bytes 9437188
  439.3 5.8 %copy-start.12 = (f32[24,2304]{1,0:T(8,128)S(1)}, f32[24,2304]{1,0:T(8,128)}, u32[]{:S(2)}) copy-start(f32[24,2304]{1,0:T(8,128)} %get-tuple-element.109) | copy-start | bytes 663556
  439.3 6.5 %copy-start.13 = (f32[24,768]{1,0:T(8,128)S(1)}, f32[24,768]{1,0:T(8,128)}, u32[]{:S(2)}) copy-start(f32[24,768]{1,0:T(8,128)} %get-tuple-element.111) | copy-start | bytes 221188
  439.3 7.1 %copy-start.11 = (f32[24,3072]{1,0:T(8,128)S(1)}, f32[24,3072]{1,0:T(8,128)}, u32[]{:S(2)}) copy-start(f32[24,3072]{1,0:T(8,128)} %get-tuple-element.115) | copy-start | bytes 884740
  439.3 7.8 %copy-start.10 = (f32[96,768]{1,0:T(8,128)S(1)}, f32[96,768]{1,0:T(8,128)}, u32[]{:S(2)}) copy-start(f32[96,768]{1,0:T(8,128)} %get-tuple-element.117) | copy-start | bytes 884740
  (8 other events, 22.5 us)
